TPU v7x, 32 devices: a whole 2x2x4 slice. The times are simulated.
32 devices in a mesh: gx: 8 (over y, x, core), gy: 4 (over z).
Axes of the slice: x: 2, y: 2, z: 4, core: 2. Of those that a mesh axis runs over, the one named last changes fastest.
Arguments:
- collocation: bfloat16 [3072, 16384], P(None, 'gx'), may hold values from -6 to 6
- density: bfloat16 [3072, 3072], P('gy'), may hold values from -0.109375 to 0.109375
- kernel: bfloat16 [16384, 8, 4, 512], P('gx', None, 'gy'), may hold values from -6.67572e-06 to 6.67572e-06
Outputs:
- exchange: float32 [3072, 3072], P('gx', 'gy')
All inputs are finite; a program needn't handle non-finite values.
Results may differ from a plain program's by a relative error of at most 0.008.
Values may be sent and summed in bfloat16 or wider, within the bound.
A program may use at most 448 MiB of HBM per device.

v0:
```python
import jax
import jax.numpy as jnp
from jax import lax
from jax.sharding import PartitionSpec as P


def local(collocation, density, kernel):
    piece_width = kernel.shape[3]
    column_group = lax.axis_index("gy")
    own_rows = jnp.dot(density, collocation, preferred_element_type=jnp.float32).astype(
        jnp.bfloat16
    )
    dense_block = lax.all_gather(own_rows, "gy", axis=0, tiled=True)
    own_piece = lax.dynamic_slice_in_dim(collocation, column_group * piece_width, piece_width, 1)
    kernel_tiles = kernel[:, :, 0, :]
    panel_rows = kernel_tiles.shape[0]
    gathered = lax.all_gather(own_piece, "gx", axis=1, tiled=True)
    products = lax.dot_general(
        dense_block, gathered, (((0,), (0,)), ((), ())), preferred_element_type=jnp.float32
    )
    coefficients = kernel_tiles.reshape(panel_rows, gathered.shape[1])
    weighted = (coefficients.astype(jnp.float32) * products).astype(jnp.bfloat16)
    chosen = gathered
    reduced_cols = lax.psum_scatter(
        lax.dot_general(
            chosen, weighted, (((1,), (1,)), ((), ())), preferred_element_type=jnp.float32
        ),
        "gy",
        scatter_dimension=0,
        tiled=True,
    ).astype(jnp.bfloat16)
    chosen = collocation
    return lax.psum_scatter(
        lax.dot_general(
            chosen, reduced_cols, (((1,), (1,)), ((), ())), preferred_element_type=jnp.float32
        ),
        "gx",
        scatter_dimension=0,
        tiled=True,
    )


def solution(mesh):
    return jax.shard_map(
        local,
        mesh=mesh,
        in_specs=(P(None, "gx"), P("gy", None), P("gx", None, "gy", None)),
        out_specs=P("gx", "gy"),
        check_vma=False,
    )
```

profile of v0, /device:TPU:0, one launch (start us, length us, event | category | flops | bytes accessed | tf_op | source)
XLA Modules:
  0.0 1016.0 jit_solution(8901126047309515792)
XLA Ops:
  6.5 0.0 all-gather.5.cloned.1.call-start
  6.5 15.4 %convolution_convert_fusion = bf16[768,2048]{1,0:T(8,128)(2,1)} fusion(bf16[768,3072]{1,0:T(8,128)(2,1)} %param.4, bf16[3072,2048]{1,0:T(8,128)(2,1)} %param.3), kind=kOutput, calls=%fused_computation.2 | convolution fusion | flops 9665249280 | bytes 20447232 | tf_op jit(solution)/shard_map/dot_general | solution.py:10
  22.0 0.0 all-gather.5.cloned.1.call-update
  22.0 0.0 all-gather.3.cloned.1.call-start
  22.0 3.8 constant_dynamic-slice_fusion
  25.8 0.0 all-gather.3.cloned.1.call-update
  25.9 0.0 reduce-scatter.3.cloned.1.call-start
  25.9 20.2 %copy.5 = f32[256,8,8,512]{3,1,2,0:T(8,128)} copy(bf16[256,8,8,512]{3,2,1,0:T(8,128)(2,1)} %bitcast.15) | data formatting | bytes 50331648
  46.1 197.0 %all-gather.5.cloned.1.call-done = bf16[3072,2048]{1,0:T(8,128)(2,1)} async-done(((bf16[768,2048]{1,0:T(8,128)(2,1)}), bf16[3072,2048]{1,0:T(8,128)(2,1)}) %all-gather.5.cloned.1.call-update) | async-done | bytes 12582928 | tf_op jit(solution)/shard_map/all_gather | solution.py:13
  243.1 130.3 %all-gather.3.cloned.1.call-done = bf16[3072,4096]{1,0:T(8,128)(2,1)} async-done(((bf16[3072,512]{1,0:T(8,128)(2,1)}), bf16[3072,4096]{1,0:T(8,128)(2,1)}) %all-gather.3.cloned.1.call-update) | async-done | bytes 25165840 | tf_op jit(solution)/shard_map/all_gather | solution.py:17
  373.3 62.4 %multiply_convert_fusion = bf16[2048,4096]{1,0:T(8,128)(2,1)} fusion(f32[2048,4096]{1,0:T(8,128)} %bitcast.14, bf16[3072,2048]{1,0:T(8,128)(2,1)} %all-gather.5.cloned.1.call-done, bf16[3072,4096]{1,0:T(8,128)(2,1)} %all-gather.3.cloned.1.call-done), kind=kOutput, calls=%fused_computation | convolution fusion | flops 51556384768 | bytes 88080384 | tf_op jit(solution)/shard_map/dot_general | solution.py:18
  435.7 61.0 %fusion.1 = f32[3072,2048]{1,0:T(8,128)} fusion(bf16[3072,4096]{1,0:T(8,128)(2,1)} %all-gather.3.cloned.1.call-done, bf16[2048,4096]{1,0:T(8,128)(2,1)} %multiply_convert_fusion), kind=kOutput, calls=%fused_computation.5 | convolution fusion | flops 51539607552 | bytes 67108864 | tf_op jit(solution)/shard_map/dot_general | solution.py:25
  496.7 0.0 reduce-scatter.3.cloned.1.call-update
  496.8 0.0 reduce-scatter.5.cloned.1.call-start
  496.8 414.3 %reduce-scatter.3.cloned.1.call-done = f32[768,2048]{1,0:T(8,128)} async-done(((f32[3072,2048]{1,0:T(8,128)}), f32[768,2048]{1,0:T(8,128)}) %reduce-scatter.3.cloned.1.call-update) | async-done | bytes 6291472 | tf_op jit(solution)/shard_map/reduce_scatter | solution.py:24
  911.1 16.9 %convolution_bitcast_fusion = f32[3072,768]{0,1:T(8,128)} fusion(bf16[3072,2048]{1,0:T(8,128)(2,1)} %param.3, f32[768,2048]{1,0:T(8,128)} %reduce-scatter.3.cloned.1.call-done), kind=kOutput, calls=%fused_computation.1 | convolution fusion | flops 9665249280 | bytes 28311552 | tf_op jit(solution)/shard_map/dot_general | solution.py:34
  928.0 0.0 reduce-scatter.5.cloned.1.call-update
  928.1 78.8 %reduce-scatter.5.cloned.1.call-done = f32[384,768]{0,1:T(8,128)} async-done(((f32[3072,768]{0,1:T(8,128)}), f32[384,768]{0,1:T(8,128)}) %reduce-scatter.5.cloned.1.call-update) | async-done | bytes 1179664 | tf_op jit(solution)/shard_map/reduce_scatter | solution.py:33
  1006.8 2.7 copy.4
Async XLA Ops:
  6.5 236.5 %all-gather.5.cloned.1.call-start = ((), (), s32[]{:S(2)}) async-start(), calls=%async_computation.3 | async-start | bytes 15728640 | tf_op jit(solution)/shard_map/all_gather | solution.py:13
  22.0 351.3 %all-gather.3.cloned.1.call-start = ((), (), s32[]{:S(2)}) async-start(), calls=%async_computation.2 | async-start | bytes 28311552 | tf_op jit(solution)/shard_map/all_gather | solution.py:17
  25.9 885.3 %reduce-scatter.3.cloned.1.call-start = ((), (), s32[]{:S(2)}) async-start(), calls=%async_computation.4 | async-start | bytes 31457280 | tf_op jit(solution)/shard_map/reduce_scatter | solution.py:24
  496.8 510.0 %reduce-scatter.5.cloned.1.call-start = ((), (), s32[]{:S(2)}) async-start(), calls=%async_computation.5 | async-start | bytes 10616832 | tf_op jit(solution)/shard_map/reduce_scatter | solution.py:33
Sparse Core Ops, SparseCore 0:
  22.1 220.8 all-gather.4
  244.9 128.3 all-gather.2
  496.9 414.1 reduce-scatter.2
  928.2 78.5 reduce-scatter.4
where the time goes:
time: 1020 us
  waiting for transfers between devices  820 us (80%)
  matrix products  156 us (15%)
  local copies, waits for them, and re-layouts  26.6 us (3%)
  between operations  13.1 us (1%)
    reduce_scatter x1, waiting for transfers between devices, local(): lax.psum_scatter(lax.dot_general(chosen, weighted, (((1,), (1,)), ((), ()...  414 us
    all_gather x1, waiting for transfers between devices, local(): dense_block = lax.all_gather(own_rows, 'gy', axis=0, tiled=True)  197 us
    all_gather x1, waiting for transfers between devices, local(): gathered = lax.all_gather(own_piece, 'gx', axis=1, tiled=True)  130 us
    reduce_scatter x1, waiting for transfers between devices, local(): lax.psum_scatter(lax.dot_general(chosen, reduced_cols, (((1,), (1,)), (()...  78.8 us
    dot_general x1, matrix products, local(): lax.dot_general(dense_block, gathered, (((0,), (0,)), ((), ())), preferre...  62.4 us
    dot_general x1, matrix products, local(): lax.dot_general(chosen, weighted, (((1,), (1,)), ((), ())), preferred_ele...  61 us
  transfers between devices with their start and end apart: 4, of which 4 were waited for; matrix products, arithmetic and copies ran while one was open for 2% of the time, Pallas kernels for 0%

commit v1 on v0

v1 whole, which is shorter than its diff:
```python
import jax
import jax.numpy as jnp
from jax import lax
from jax.sharding import PartitionSpec as P

F32 = jnp.float32
BF16 = jnp.bfloat16


def spread(block, axis_size, axis):
    rows = block.shape[0]
    me = lax.axis_index("gy")
    out = jnp.zeros((axis_size * rows, block.shape[1]), block.dtype)
    out = lax.dynamic_update_slice_in_dim(out, block, me * rows, 0)
    for shift in range(1, axis_size):
        pairs = [(k, (k + shift) % axis_size) for k in range(axis_size)]
        got = lax.ppermute(block, axis, pairs)
        source = lax.rem(me + axis_size - shift, axis_size)
        out = lax.dynamic_update_slice_in_dim(out, got, source * rows, 0)
    return out


def exchange_sum(part, axis_size, axis):
    width = part.shape[1] // axis_size
    me = lax.axis_index(axis)
    total = lax.dynamic_slice_in_dim(part, me * width, width, 1).astype(F32)
    for shift in range(1, axis_size):
        pairs = [(k, (k + shift) % axis_size) for k in range(axis_size)]
        target = lax.rem(me + shift, axis_size)
        sent = lax.dynamic_slice_in_dim(part, target * width, width, 1)
        total = total + lax.ppermute(sent, axis, pairs).astype(F32)
    return total


def build(n_gx, n_gy):
    def local(collocation, density, kernel):
        nbf, panel_rows = collocation.shape
        piece = kernel.shape[3]
        i, j = lax.axis_index("gx"), lax.axis_index("gy")
        halves = 2 if piece % 256 == 0 else 1
        half = piece // halves
        own = [
            lax.dynamic_slice_in_dim(collocation, j * piece + h * half, half, 1)
            for h in range(halves)
        ]
        gathered = [lax.all_gather(own[0], "gx", axis=1, tiled=True)]

        cols = nbf // n_gx
        strip = spread(lax.dynamic_slice_in_dim(density, i * cols, cols, 1), n_gy, "gy")
        whole = lax.all_gather(strip, "gx", axis=0, tiled=False)
        for h in range(1, halves):
            later, whole = lax.optimization_barrier((own[h], whole))
            gathered.append(lax.all_gather(later, "gx", axis=1, tiled=True))
        dense = lax.dot_general(
            whole,
            collocation.reshape(n_gx, cols, panel_rows),
            (((0, 2), (0, 1)), ((), ())),
            preferred_element_type=F32,
        ).astype(BF16)

        weighted = []
        for h in range(halves):
            tile = kernel[:, :, 0, h * half : (h + 1) * half].reshape(panel_rows, -1)
            products = lax.dot_general(
                dense, gathered[h], (((0,), (0,)), ((), ())), preferred_element_type=F32
            )
            weighted.append((tile.astype(F32) * products).astype(BF16))

        parts = 3 if (nbf // n_gy) % 384 == 0 else 1
        sub = nbf // n_gy // parts
        done = []
        for c in range(parts):
            contracted = 0.0
            for h in range(halves):
                rows = gathered[h].reshape(n_gy, parts, sub, -1)[:, c].reshape(n_gy * sub, -1)
                contracted = contracted + lax.dot_general(
                    rows, weighted[h], (((1,), (1,)), ((), ())), preferred_element_type=F32
                )
            term = lax.dot_general(
                collocation,
                contracted.astype(BF16),
                (((1,), (1,)), ((), ())),
                preferred_element_type=F32,
            ).astype(BF16)
            summed = lax.psum_scatter(term, "gx", scatter_dimension=0, tiled=True)
            done.append(exchange_sum(summed, n_gy, "gy"))
        return jnp.concatenate(done, axis=1)

    return local


def solution(mesh):
    return jax.shard_map(
        build(mesh.shape["gx"], mesh.shape["gy"]),
        mesh=mesh,
        in_specs=(P(None, "gx"), P("gy", None), P("gx", None, "gy", None)),
        out_specs=P("gx", "gy"),
        check_vma=False,
    )
```

time: 1020 us -> 613 us (0.60)
  waiting for transfers between devices: 820 us -> 196 us
  matrix products: 156 us -> 254 us
  local copies, waits for them, and re-layouts: 26.6 us -> 92.3 us
  starting transfers between devices: 0.13 us -> 35.5 us
  other arithmetic: 0 us -> 12.5 us
    reduce_scatter x2 -> x0, waiting for transfers between devices: 493 us -> none  [the longest x1 414 us: local(): lax.psum_scatter(lax.dot_general(chosen, weighted, (((1,), (1,)), ((), ()...]
    all_gather x2 -> x3, waiting for transfers between devices: 327 us -> 79.2 us  [the longest x1 79.2 us: local(): whole = lax.all_gather(strip, 'gx', axis=0, tiled=False)]
    dot_general x4 -> x12, matrix products: 156 us -> 254 us  [the longest x6 89.1 us: local(): lax.dot_general(rows, weighted[h], (((1,), (1,)), ((), ())), preferred_el...]
    unnamed x4 -> x9, waiting for transfers between devices: 0.07 us -> 72.4 us
    ppermute x0 -> x12, waiting for transfers between devices: none -> 44.6 us  [the longest x3 35.8 us: spread(): got = lax.ppermute(block, axis, pairs)]
    unnamed x1 -> x39, local copies, waits for them, and re-layouts: 20.2 us -> 61.5 us
    ppermute x0 -> x12, starting transfers between devices: none -> 35.2 us  [the longest x9 28.1 us: exchange_sum(): total = total + lax.ppermute(sent, axis, pairs).astype(F32)]
    slice x0 -> x2, local copies, waits for them, and re-layouts: none -> 18.9 us  [local(): gathered[h].reshape(n_gy, parts, sub, -1)[:, c].reshape(n_gy * sub, -1)]
  transfers between devices with their start and end apart: 4 -> 18, of which waited for: 4 -> 6; matrix products, arithmetic and copies ran while one was open for 2% -> 44% of each run, Pallas kernels for 0% -> 0%
where the time goes in v1:
time: 613 us; the launch traced here: 604 us
  matrix products  254 us (41%)
  waiting for transfers between devices  196 us (32%)
  local copies, waits for them, and re-layouts  92.3 us (15%)
  starting transfers between devices  35.5 us (6%)
  between operations  14 us (2%)
  other arithmetic  12.5 us (2%)
    dot_general x6, matrix products, local(): lax.dot_general(rows, weighted[h], (((1,), (1,)), ((), ())), preferred_el...  89.1 us
    all_gather x1, waiting for transfers between devices, local(): whole = lax.all_gather(strip, 'gx', axis=0, tiled=False)  79.2 us
    unnamed x9, waiting for transfers between devices  72.4 us
    dot_general x2, matrix products, local(): lax.dot_general(dense, gathered[h], (((0,), (0,)), ((), ())), preferred_e...  67.8 us
    unnamed x39, local copies, waits for them, and re-layouts  61.5 us
    dot_general x3, matrix products, local(): lax.dot_general(collocation, contracted.astype(BF16), (((1,), (1,)), ((),...  50.9 us
    dot_general x1, matrix products, local(): lax.dot_general(whole, collocation.reshape(n_gx, cols, panel_rows), (((0,...  46.2 us
    ppermute x3, waiting for transfers between devices, spread(): got = lax.ppermute(block, axis, pairs)  35.8 us
  transfers between devices with their start and end apart: 18, of which 6 were waited for; matrix products, arithmetic and copies ran while one was open for 44% of the time, Pallas kernels for 0%

profile of v1, /device:TPU:0, one launch (start us, length us, event | category | flops | bytes accessed | tf_op | source)
XLA Modules:
  0.0 604.5 jit_solution(4618804121003561843)
XLA Ops:
  6.5 3.8 constant_dynamic-slice_fusion.13
  11.9 3.1 collective-permute-start
  15.0 2.6 collective-permute-start.1
  18.9 12.5 %collective-permute-done = bf16[768,384]{1,0:T(8,128)(2,1)} collective-permute-done((bf16[768,384]{1,0:T(8,128)(2,1)S(1)}, bf16[768,384]{1,0:T(8,128)(2,1)}, u32[]{:S(2)}, u32[]{:S(2)}) %collective-permute-start) | collective-permute-done | bytes 589856 | tf_op jit(solution)/shard_map/ppermute | solution.py:17
  32.6 23.3 %collective-permute-done.1 = bf16[768,384]{1,0:T(8,128)(2,1)} collective-permute-done((bf16[768,384]{1,0:T(8,128)(2,1)S(1)}, bf16[768,384]{1,0:T(8,128)(2,1)}, u32[]{:S(2)}, u32[]{:S(2)}) %collective-permute-start.1) | collective-permute-done | bytes 589856 | tf_op jit(solution)/shard_map/ppermute | solution.py:17
  58.6 12.2 %slice_convert_fusion = (f32[2048,8,1,256]{3,1,2,0:T(8,128)}, f32[2048,8,1,256]{3,1,2,0:T(8,128)S(1)}) fusion(bf16[2048,8,1,512]{3,1,2,0:T(8,128)(2,1)} %param.5), kind=kLoop, calls=%fused_computation.6 | loop fusion | flops 8388608 | bytes 50331648 | tf_op jit(solution)/shard_map/convert_element_type | solution.py:67
  70.8 15.8 %copy.25 = f32[256,8,8,256]{3,1,2,0:T(8,128)} copy(f32[256,8,8,256]{3,2,1,0:T(8,128)} %bitcast.73) | data formatting | bytes 33554432
  86.6 11.6 %copy.24 = f32[256,8,8,256]{3,1,2,0:T(8,128)} copy(f32[256,8,8,256]{3,2,1,0:T(8,128)S(1)} %bitcast.72) | data formatting | bytes 33554432
  98.1 10.8 %fusion.7 = (bf16[4,1,256,2048]{3,2,1,0:T(8,128)(2,1)}, bf16[4,1,256,2048]{3,2,1,0:T(8,128)(2,1)}, bf16[4,1,256,2048]{3,2,1,0:T(8,128)(2,1)}) fusion(bf16[4,3,256,2048]{3,2,1,0:T(8,128)(2,1)} %bitcast.76), kind=kLoop, calls=%fused_computation.38 | loop fusion | bytes 25165824 | tf_op jit(solution)/shard_map/slice | solution.py:75
  109.0 79.2 %all-gather.6.cloned.1.call-done = bf16[8,3072,384]{2,1,0:T(8,128)(2,1)} async-done(((bf16[1,3072,384]{2,1,0:T(8,128)(2,1)}), bf16[8,3072,384]{2,1,0:T(8,128)(2,1)}) %all-gather.6.cloned.1.call-update) | async-done | bytes 18874384 | tf_op jit(solution)/shard_map/all_gather | solution.py:50
  188.5 46.2 %bitcast_convert_fusion = bf16[3072,2048]{1,0:T(8,128)(2,1)} fusion(bf16[8,3072,384]{2,1,0:T(8,128)(2,1)} %all-gather.6.cloned.1.call-done, bf16[8,384,2048]{2,1,0:T(8,128)(2,1)} %bitcast.84), kind=kOutput, calls=%fused_computation | convolution fusion | flops 38660997120 | bytes 44040192 | tf_op jit(solution)/shard_map/dot_general | solution.py:54
  234.6 34.7 %multiply_convert_fusion.1 = bf16[2048,2048]{1,0:T(8,128)(2,1)} fusion(f32[2048,2048]{1,0:T(8,128)S(1)} %bitcast.75, bf16[3072,2048]{1,0:T(8,128)(2,1)} %bitcast_convert_fusion, bf16[3072,2048]{1,0:T(8,128)(2,1)} %all-gather.4.cloned.1.call-done), kind=kOutput, calls=%fused_computation.2 | convolution fusion | flops 25778192384 | bytes 50331648 | tf_op jit(solution)/shard_map/dot_general | solution.py:64
  269.3 14.7 %fusion.8 = f32[1024,2048]{1,0:T(8,128)} fusion(bf16[1024,2048]{1,0:T(8,128)(2,1)} %bitcast.82, bf16[2048,2048]{1,0:T(8,128)(2,1)} %multiply_convert_fusion.1), kind=kOutput, calls=%fused_computation.39 | convolution fusion | flops 8589934592 | bytes 20971520 | tf_op jit(solution)/shard_map/dot_general | solution.py:76
  284.0 8.1 %fusion.6 = (bf16[4,1,256,2048]{3,2,1,0:T(8,128)(2,1)S(1)}, bf16[4,1,256,2048]{3,2,1,0:T(8,128)(2,1)}, bf16[4,1,256,2048]{3,2,1,0:T(8,128)(2,1)}) fusion(bf16[4,3,256,2048]{3,2,1,0:T(8,128)(2,1)} %bitcast.77), kind=kLoop, calls=%fused_computation.37 | loop fusion | bytes 25165824 | tf_op jit(solution)/shard_map/slice | solution.py:75
  292.1 3.1 copy-done.1
  295.2 33.1 %multiply_convert_fusion = bf16[2048,2048]{1,0:T(8,128)(2,1)} fusion(f32[2048,2048]{1,0:T(8,128)} %bitcast.74, bf16[3072,2048]{1,0:T(8,128)(2,1)} %bitcast_convert_fusion, bf16[3072,2048]{1,0:T(8,128)(2,1)S(1)} %copy-done.1), kind=kOutput, calls=%fused_computation.1 | convolution fusion | flops 25778192384 | bytes 50331648 | tf_op jit(solution)/shard_map/dot_general | solution.py:64
  328.2 13.2 %add_convert_fusion.10 = bf16[1024,2048]{1,0:T(8,128)(2,1)S(1)} fusion(f32[1024,2048]{1,0:T(8,128)} %fusion.8, bf16[1024,2048]{1,0:T(8,128)(2,1)S(1)} %bitcast.83, bf16[2048,2048]{1,0:T(8,128)(2,1)} %multiply_convert_fusion), kind=kOutput, calls=%fused_computation.5.clone.clone | convolution fusion | flops 8594128896 | bytes 25165824 | tf_op jit(solution)/shard_map/dot_general | solution.py:76
  341.5 17.5 %convert_bitcast_fusion.2 = bf16[3072,1024]{0,1:T(8,128)(2,1)} fusion(bf16[3072,2048]{1,0:T(8,128)(2,1)} %param.3, bf16[1024,2048]{1,0:T(8,128)(2,1)S(1)} %add_convert_fusion.10), kind=kOutput, calls=%fused_computation.10 | convolution fusion | flops 12888047616 | bytes 23068672 | tf_op jit(solution)/shard_map/dot_general | solution.py:79
  358.9 8.6 %copy.6 = bf16[3072,1024]{1,0:T(8,128)(2,1)} copy(bf16[3072,1024]{0,1:T(8,128)(2,1)} %convert_bitcast_fusion.2) | data formatting | bytes 12582912
  367.6 14.8 %fusion.9 = f32[1024,2048]{1,0:T(8,128)} fusion(bf16[1024,2048]{1,0:T(8,128)(2,1)} %bitcast.79, bf16[2048,2048]{1,0:T(8,128)(2,1)} %multiply_convert_fusion.1), kind=kOutput, calls=%fused_computation.40 | convolution fusion | flops 8589934592 | bytes 20971520 | tf_op jit(solution)/shard_map/dot_general | solution.py:76
  382.4 15.3 %add_convert_fusion.9 = bf16[1024,2048]{1,0:T(8,128)(2,1)} fusion(f32[1024,2048]{1,0:T(8,128)} %fusion.9, bf16[1024,2048]{1,0:T(8,128)(2,1)S(1)} %bitcast.81, bf16[2048,2048]{1,0:T(8,128)(2,1)} %multiply_convert_fusion), kind=kOutput, calls=%fused_computation.4.clone.clone | convolution fusion | flops 8594128896 | bytes 25165824 | tf_op jit(solution)/shard_map/dot_general | solution.py:76
  397.7 16.7 %convert_bitcast_fusion.1 = bf16[3072,1024]{0,1:T(8,128)(2,1)} fusion(bf16[3072,2048]{1,0:T(8,128)(2,1)S(1)} %bitcast.86, bf16[1024,2048]{1,0:T(8,128)(2,1)} %add_convert_fusion.9), kind=kOutput, calls=%fused_computation.9 | convolution fusion | flops 12888047616 | bytes 23068672 | tf_op jit(solution)/shard_map/dot_general | solution.py:79
  414.4 8.5 %copy.8 = bf16[3072,1024]{1,0:T(8,128)(2,1)} copy(bf16[3072,1024]{0,1:T(8,128)(2,1)} %convert_bitcast_fusion.1) | data formatting | bytes 12582912
  423.0 14.9 %fusion.10 = f32[1024,2048]{1,0:T(8,128)} fusion(bf16[1024,2048]{1,0:T(8,128)(2,1)} %bitcast.78, bf16[2048,2048]{1,0:T(8,128)(2,1)} %multiply_convert_fusion.1), kind=kOutput, calls=%fused_computation.41 | convolution fusion | flops 8589934592 | bytes 20971520 | tf_op jit(solution)/shard_map/dot_general | solution.py:76
  437.9 16.2 %add_convert_fusion.8 = bf16[1024,2048]{1,0:T(8,128)(2,1)} fusion(f32[1024,2048]{1,0:T(8,128)} %fusion.10, bf16[1024,2048]{1,0:T(8,128)(2,1)S(1)} %bitcast.80, bf16[2048,2048]{1,0:T(8,128)(2,1)} %multiply_convert_fusion), kind=kOutput, calls=%fused_computation.3.clone.clone.1 | convolution fusion | flops 8594128896 | bytes 25165824 | tf_op jit(solution)/shard_map/dot_general | solution.py:76
  454.1 16.7 %convert_bitcast_fusion = bf16[3072,1024]{0,1:T(8,128)(2,1)} fusion(bf16[3072,2048]{1,0:T(8,128)(2,1)S(1)} %bitcast.88, bf16[1024,2048]{1,0:T(8,128)(2,1)} %add_convert_fusion.8), kind=kOutput, calls=%fused_computation.8 | convolution fusion | flops 12888047616 | bytes 23068672 | tf_op jit(solution)/shard_map/dot_general | solution.py:79
  470.9 8.6 %copy.10 = bf16[3072,1024]{1,0:T(8,128)(2,1)} copy(bf16[3072,1024]{0,1:T(8,128)(2,1)} %convert_bitcast_fusion) | data formatting | bytes 12582912
  483.0 2.5 collective-permute-start.4
  487.3 7.2 %reduce-scatter.12.cloned.1.call-done = bf16[384,1024]{1,0:T(8,128)(2,1)} async-done(((bf16[3072,1024]{1,0:T(8,128)(2,1)}), bf16[384,1024]{1,0:T(8,128)(2,1)}) %reduce-scatter.12.cloned.1.call-update) | async-done | bytes 786448
  494.5 65.0 %reduce-scatter.14.cloned.1.call-done = bf16[384,1024]{1,0:T(8,128)(2,1)} async-done(((bf16[3072,1024]{1,0:T(8,128)(2,1)}), bf16[384,1024]{1,0:T(8,128)(2,1)}) %reduce-scatter.14.cloned.1.call-update) | async-done | bytes 786448
  572.9 14.1 %collective-permute-start.9 = (bf16[384,256]{0,1:T(8,128)(2,1)S(1)}, bf16[384,256]{0,1:T(8,128)(2,1)S(1)}, u32[]{:S(2)}, u32[]{:S(2)}) collective-permute-start(bf16[384,256]{0,1:T(8,128)(2,1)S(1)} %copy.21), channel_id=1, source_target_pairs={{0,1},{1,2},{2,3},{3,0},{4,5},{5,6},{6,7},{7,4},{8,9},{9,10},{10,1... | collective-permute-start | bytes 589832 | tf_op jit(solution)/shard_map/ppermute | solution.py:31
  587.0 8.8 %collective-permute-done.10 = bf16[384,256]{0,1:T(8,128)(2,1)S(1)} collective-permute-done((bf16[384,256]{0,1:T(8,128)(2,1)S(1)}, bf16[384,256]{0,1:T(8,128)(2,1)S(1)}, u32[]{:S(2)}, u32[]{:S(2)}) %collective-permute-start.10) | collective-permute-done | bytes 196640 | tf_op jit(solution)/shard_map/ppermute | solution.py:31
  (79 shorter events, 27.3 us)
Async XLA Ops:
  6.5 91.6 %all-gather.4.cloned.1.call-start = ((), (), s32[]{:S(2)}) async-start(), calls=%async_computation.3 | async-start | bytes 14155776 | tf_op jit(solution)/shard_map/all_gather | solution.py:46
  10.4 177.8 %all-gather.6.cloned.1.call-start = ((), (), s32[]{:S(2)}) async-start(), calls=%async_computation.4 | async-start | bytes 21233664 | tf_op jit(solution)/shard_map/all_gather | solution.py:50
  11.9 19.6 %collective-permute-start = (bf16[768,384]{1,0:T(8,128)(2,1)S(1)}, bf16[768,384]{1,0:T(8,128)(2,1)}, u32[]{:S(2)}, u32[]{:S(2)}) collective-permute-start(bf16[768,384]{1,0:T(8,128)(2,1)S(1)} %get-tuple-element.10), channel_id=1, source_target_pairs={{0,1},{1,2},{2,3},{3,0},{4,5},{5,6},{6,7},{7,4},{8,9},{9,10},{10,1... | collective-permute-start | bytes 1769480 | tf_op jit(solution)/shard_map/ppermute | solution.py:17
  15.0 40.9 %collective-permute-start.1 = (bf16[768,384]{1,0:T(8,128)(2,1)S(1)}, bf16[768,384]{1,0:T(8,128)(2,1)}, u32[]{:S(2)}, u32[]{:S(2)}) collective-permute-start(bf16[768,384]{1,0:T(8,128)(2,1)S(1)} %get-tuple-element.10), channel_id=1, source_target_pairs={{0,2},{1,3},{2,0},{3,1},{4,6},{5,7},{6,4},{7,5},{8,10},{9,11},{10,... | collective-permute-start | bytes 1769480 | tf_op jit(solution)/shard_map/ppermute | solution.py:17
  17.6 39.4 %collective-permute-start.2 = (bf16[768,384]{1,0:T(8,128)(2,1)S(1)}, bf16[768,384]{1,0:T(8,128)(2,1)S(1)}, u32[]{:S(2)}, u32[]{:S(2)}) collective-permute-start(bf16[768,384]{1,0:T(8,128)(2,1)S(1)} %get-tuple-element.10), channel_id=1, source_target_pairs={{0,3},{1,0},{2,1},{3,2},{4,7},{5,4},{6,5},{7,6},{8,11},{9,8},{10,9... | collective-permute-start | bytes 1769480 | tf_op jit(solution)/shard_map/ppermute | solution.py:17
  57.1 1.4 copy-start.2
  58.6 225.4 %all-gather.8.cloned.1.call-start = ((), (), s32[]{:S(2)}) async-start(), calls=%async_computation.5 | async-start | bytes 14155776 | tf_op jit(solution)/shard_map/all_gather | solution.py:53
  188.2 291.3 %reduce-scatter.10.cloned.1.call-start = ((), (), s32[]{:S(2)}) async-start(), calls=%async_computation.6 | async-start | bytes 7077888
  188.4 46.2 %copy-start = (f32[256,8,8,256]{3,1,2,0:T(8,128)S(1)}, f32[256,8,8,256]{3,1,2,0:T(8,128)}, u32[]{:S(2)}) copy-start(f32[256,8,8,256]{3,1,2,0:T(8,128)} %copy.24) | copy-start | bytes 50331652
  284.0 11.1 %copy-start.1 = (bf16[3072,2048]{1,0:T(8,128)(2,1)S(1)}, bf16[3072,2048]{1,0:T(8,128)(2,1)}, u32[]{:S(2)}) copy-start(bf16[3072,2048]{1,0:T(8,128)(2,1)} %all-gather.8.cloned.1.call-done) | copy-start | bytes 37748740
  367.5 126.9 %reduce-scatter.12.cloned.1.call-start = ((), (), s32[]{:S(2)}) async-start(), calls=%async_computation.7 | async-start | bytes 7077888
  367.6 14.8 %copy-start.4 = (bf16[4,1,256,2048]{3,2,1,0:T(8,128)(2,1)S(1)}, bf16[4,1,256,2048]{3,2,1,0:T(8,128)(2,1)}, u32[]{:S(2)}) copy-start(bf16[4,1,256,2048]{3,2,1,0:T(8,128)(2,1)} %get-tuple-element.15) | copy-start | bytes 12582916
  367.6 30.1 %slice-start = ((s8[12582912]{0:T(1024)(128)(4,1)}), s8[4194304]{0:T(1024)(128)(4,1)S(1)}, s32[]{:S(2)}) async-start(s8[12582912]{0:T(1024)(128)(4,1)} %bitcast.85), calls=%async_computation.9 | async-start | bytes 8388608
  367.6 30.1 %slice-start.1 = ((s8[12582912]{0:T(1024)(128)(4,1)}), s8[4194304]{0:T(1024)(128)(4,1)S(1)}, s32[]{:S(2)}) async-start(s8[12582912]{0:T(1024)(128)(4,1)} %bitcast.85), calls=%async_computation.10 | async-start | bytes 8388608
  382.4 15.3 %slice-start.2 = ((s8[12582912]{0:T(1024)(128)(4,1)}), s8[4194304]{0:T(1024)(128)(4,1)S(1)}, s32[]{:S(2)}) async-start(s8[12582912]{0:T(1024)(128)(4,1)} %bitcast.85), calls=%async_computation.11 | async-start | bytes 8388608
  422.9 136.6 %reduce-scatter.14.cloned.1.call-start = ((), (), s32[]{:S(2)}) async-start(), calls=%async_computation.8 | async-start | bytes 7077888
  423.0 14.9 %copy-start.3 = (bf16[4,1,256,2048]{3,2,1,0:T(8,128)(2,1)S(1)}, bf16[4,1,256,2048]{3,2,1,0:T(8,128)(2,1)}, u32[]{:S(2)}) copy-start(bf16[4,1,256,2048]{3,2,1,0:T(8,128)(2,1)} %get-tuple-element.14) | copy-start | bytes 12582916
  423.0 31.1 %slice-start.3 = ((s8[12582912]{0:T(1024)(128)(4,1)}), s8[4194304]{0:T(1024)(128)(4,1)S(1)}, s32[]{:S(2)}) async-start(s8[12582912]{0:T(1024)(128)(4,1)} %bitcast.87), calls=%async_computation.12 | async-start | bytes 8388608
  423.0 31.1 %slice-start.4 = ((s8[12582912]{0:T(1024)(128)(4,1)}), s8[4194304]{0:T(1024)(128)(4,1)S(1)}, s32[]{:S(2)}) async-start(s8[12582912]{0:T(1024)(128)(4,1)} %bitcast.87), calls=%async_computation.13 | async-start | bytes 8388608
  437.9 16.2 %slice-start.5 = ((s8[12582912]{0:T(1024)(128)(4,1)}), s8[4194304]{0:T(1024)(128)(4,1)S(1)}, s32[]{:S(2)}) async-start(s8[12582912]{0:T(1024)(128)(4,1)} %bitcast.87), calls=%async_computation.14 | async-start | bytes 8388608
  481.0 87.3 %collective-permute-start.3 = (bf16[384,256]{0,1:T(8,128)(2,1)S(1)}, bf16[384,256]{0,1:T(8,128)(2,1)S(1)}, u32[]{:S(2)}, u32[]{:S(2)}) collective-permute-start(bf16[384,256]{0,1:T(8,128)(2,1)S(1)} %copy.13), channel_id=1, source_target_pairs={{0,1},{1,2},{2,3},{3,0},{4,5},{5,6},{6,7},{7,4},{8,9},{9,10},{10,1... | collective-permute-start | bytes 589832 | tf_op jit(solution)/shard_map/ppermute | solution.py:31
  483.0 86.8 %collective-permute-start.4 = (bf16[384,256]{0,1:T(8,128)(2,1)S(1)}, bf16[384,256]{0,1:T(8,128)(2,1)S(1)}, u32[]{:S(2)}, u32[]{:S(2)}) collective-permute-start(bf16[384,256]{0,1:T(8,128)(2,1)S(1)} %copy.14), channel_id=1, source_target_pairs={{0,2},{1,3},{2,0},{3,1},{4,6},{5,7},{6,4},{7,5},{8,10},{9,11},{10,... | collective-permute-start | bytes 589832 | tf_op jit(solution)/shard_map/ppermute | solution.py:31
  485.6 84.7 %collective-permute-start.5 = (bf16[384,256]{0,1:T(8,128)(2,1)S(1)}, bf16[384,256]{0,1:T(8,128)(2,1)S(1)}, u32[]{:S(2)}, u32[]{:S(2)}) collective-permute-start(bf16[384,256]{0,1:T(8,128)(2,1)S(1)} %copy.15), channel_id=1, source_target_pairs={{0,3},{1,0},{2,1},{3,2},{4,7},{5,4},{6,5},{7,6},{8,11},{9,8},{10,9... | collective-permute-start | bytes 589832 | tf_op jit(solution)/shard_map/ppermute | solution.py:31
  561.9 10.9 %collective-permute-start.6 = (bf16[384,256]{0,1:T(8,128)(2,1)}, bf16[384,256]{0,1:T(8,128)(2,1)S(1)}, u32[]{:S(2)}, u32[]{:S(2)}) collective-permute-start(bf16[384,256]{0,1:T(8,128)(2,1)} %copy.17), channel_id=1, source_target_pairs={{0,1},{1,2},{2,3},{3,0},{4,5},{5,6},{6,7},{7,4},{8,9},{9,10},{10,1... | collective-permute-start | bytes 589832 | tf_op jit(solution)/shard_map/ppermute | solution.py:31
  564.2 22.7 %collective-permute-start.7 = (bf16[384,256]{0,1:T(8,128)(2,1)}, bf16[384,256]{0,1:T(8,128)(2,1)S(1)}, u32[]{:S(2)}, u32[]{:S(2)}) collective-permute-start(bf16[384,256]{0,1:T(8,128)(2,1)} %copy.18), channel_id=1, source_target_pairs={{0,2},{1,3},{2,0},{3,1},{4,6},{5,7},{6,4},{7,5},{8,10},{9,11},{10,... | collective-permute-start | bytes 589832 | tf_op jit(solution)/shard_map/ppermute | solution.py:31
  568.3 18.6 %collective-permute-start.8 = (bf16[384,256]{0,1:T(8,128)(2,1)}, bf16[384,256]{0,1:T(8,128)(2,1)S(1)}, u32[]{:S(2)}, u32[]{:S(2)}) collective-permute-start(bf16[384,256]{0,1:T(8,128)(2,1)} %copy.19), channel_id=1, source_target_pairs={{0,3},{1,0},{2,1},{3,2},{4,7},{5,4},{6,5},{7,6},{8,11},{9,8},{10,9... | collective-permute-start | bytes 589832 | tf_op jit(solution)/shard_map/ppermute | solution.py:31
  569.8 26.0 %collective-permute-start.10 = (bf16[384,256]{0,1:T(8,128)(2,1)S(1)}, bf16[384,256]{0,1:T(8,128)(2,1)S(1)}, u32[]{:S(2)}, u32[]{:S(2)}) collective-permute-start(bf16[384,256]{0,1:T(8,128)(2,1)S(1)} %copy.22), channel_id=1, source_target_pairs={{0,2},{1,3},{2,0},{3,1},{4,6},{5,7},{6,4},{7,5},{8,10},{9,11},{10,... | collective-permute-start | bytes 589832 | tf_op jit(solution)/shard_map/ppermute | solution.py:31
  570.3 25.5 %collective-permute-start.11 = (bf16[384,256]{0,1:T(8,128)(2,1)S(1)}, bf16[384,256]{0,1:T(8,128)(2,1)S(1)}, u32[]{:S(2)}, u32[]{:S(2)}) collective-permute-start(bf16[384,256]{0,1:T(8,128)(2,1)S(1)} %copy.23), channel_id=1, source_target_pairs={{0,3},{1,0},{2,1},{3,2},{4,7},{5,4},{6,5},{7,6},{8,11},{9,8},{10,9... | collective-permute-start | bytes 589832 | tf_op jit(solution)/shard_map/ppermute | solution.py:31
  572.9 23.0 %collective-permute-start.9 = (bf16[384,256]{0,1:T(8,128)(2,1)S(1)}, bf16[384,256]{0,1:T(8,128)(2,1)S(1)}, u32[]{:S(2)}, u32[]{:S(2)}) collective-permute-start(bf16[384,256]{0,1:T(8,128)(2,1)S(1)} %copy.21), channel_id=1, source_target_pairs={{0,1},{1,2},{2,3},{3,0},{4,5},{5,6},{6,7},{7,4},{8,9},{9,10},{10,1... | collective-permute-start | bytes 589832 | tf_op jit(solution)/shard_map/ppermute | solution.py:31
Sparse Core Ops, SparseCore 0:
  10.5 77.1 all-gather.3
  89.6 98.5 all-gather.5
  190.1 74.4 all-gather.7
  367.7 61.7 reduce-scatter.9
  432.7 61.7 reduce-scatter.11
  497.7 61.7 reduce-scatter.13
